TPU v7x, 32 devices: a whole 2x2x4 slice. The times are simulated.
32 devices in a mesh: grp: 8 (over z, core), blk: 4 (over y, x).
Axes of the slice: x: 2, y: 2, z: 4, core: 2. Of those that a mesh axis runs over, the one named last changes fastest.
Arguments:
- integrals: bfloat16 [8, 128, 128, 128], P(None, 'blk'), may hold values from -0.5 to 0.5
- doubles: bfloat16 [64, 128, 128], P('blk'), may hold values from -0.0059814453 to 0.0059814453
- coulomb: bfloat16 [64, 128, 128], P('blk'), may hold values from -0.1796875 to 0.1796875
- singles: float32 [8, 128], P(None, 'blk'), may hold values from -0.18 to 0.18
- occ_energy: float32 [8], replicated, may hold values from -2 to -0.5
- vir_energy: float32 [128], replicated, may hold values from 0.3 to 3
- triplets: int32 [8, 16, 3], P('grp'), may hold values from 0 to 7
- tile_count: int32 [8], P('grp'), may hold values from 1 to 16, as said below
Outputs:
- triplet_energy: float32 [8, 16], P('grp')
- mean_energy: float32 [], replicated
Inputs may be any that keep to these rules, and one draw needn't show every extreme that they name: `tile_count`: slots with an index below a group's count are live; some group has all 16 slots live.
All inputs are finite; a program needn't handle non-finite values.
Results may differ from a plain program's by a relative error of at most 0.0003.
Values may be sent and summed in bfloat16 or wider, within the bound.
A program may use at most 64 MiB of HBM per device.

v0:
```python
import functools

import jax
import jax.numpy as jnp
from jax import lax
from jax.experimental import pallas as pl
from jax.experimental.pallas import tpu as pltpu
from jax.sharding import PartitionSpec as P

MESH = pl.DeviceIdType.MESH


def team_count(occupied, rows, groups):
    teams = occupied
    while teams > 1 and (occupied % teams or rows % teams or groups % (2 * teams)):
        teams -= 1
    return teams


def gather_kernel(n, groups, teams, occupied, slots, doubles_ref, coulomb_ref, integrals_ref, trip_hbm, live_ref, dp_ref, cp_ref,
                  held_ref, list_ref, count_ref, all_ref, trip_ref, small_sem, held_sem, local_sem, send_sem, recv_sem, fsend_sem, frecv_sem, csend_sem, crecv_sem):
    g = lax.axis_index("grp")
    q = lax.axis_index("blk")
    rows, width = doubles_ref.shape[0], doubles_ref.shape[1]
    runs = rows // teams
    half = width // 2
    team = g // (groups // teams)
    core = g % 2
    partner = g + 1 - 2 * core
    mine = pl.ds(pl.multiple_of(core * half, half), half)
    arrays = ((doubles_ref, dp_ref), (coulomb_ref, cp_ref))

    barrier = pltpu.get_barrier_semaphore()
    for dg in range(1, groups):
        pl.semaphore_signal(barrier, inc=1, device_id={"grp": (g + dg) % groups}, device_id_type=MESH)
    for dq in range(1, n):
        pl.semaphore_signal(barrier, inc=1, device_id={"blk": (q + dq) % n}, device_id_type=MESH)

    def own_row(m):
        j = (q * rows + teams * m) // occupied
        return teams * m + (team + occupied * teams - j) % teams

    small = pltpu.make_async_copy(trip_hbm, trip_ref, small_sem)
    small.start()
    locals_ = []
    for m in range(runs):
        for x, (src, dst) in enumerate(arrays):
            copy = pltpu.make_async_copy(src.at[own_row(m)], dst.at[q * runs + m], local_sem.at[m, x])
            copy.start()
            locals_.append(copy)
    share = held_ref.shape[1]
    held = pltpu.make_async_copy(integrals_ref.at[:, pl.ds(core * share, share)], held_ref, held_sem)
    held.start()
    small.wait()
    i, j, k = trip_ref[0], trip_ref[1], trip_ref[2]
    cube = occupied * occupied * occupied
    owner = lax.rem(j + k, jnp.full_like(j, teams))
    code = owner * cube + (i * occupied + j) * occupied + k
    live = lax.broadcasted_iota(jnp.int32, code.shape, 1) < live_ref[0]
    all_ref[g] = jnp.full((1, all_ref.shape[2]), -1, jnp.int32)
    all_ref[g, :, :slots] = jnp.where(live, code, -1)
    pl.semaphore_wait(barrier, groups - 1 + n - 1)

    code_copies = []
    for dg in range(1, groups):
        copy = pltpu.make_async_remote_copy(
            src_ref=all_ref.at[g], dst_ref=all_ref.at[g], send_sem=csend_sem.at[dg - 1], recv_sem=crecv_sem.at[dg - 1],
            device_id={"grp": (g + dg) % groups}, device_id_type=MESH)
        copy.start()
        code_copies.append(copy)
    sends = []
    for m in range(runs):
        for x, (src, dst) in enumerate(arrays):
            locals_[m * 2 + x].wait()
            for dq in range(1, n):
                copy = pltpu.make_async_remote_copy(
                    src_ref=dst.at[q * runs + m, mine], dst_ref=dst.at[q * runs + m, mine],
                    send_sem=send_sem.at[m, x, dq - 1], recv_sem=recv_sem.at[m, x, dq - 1],
                    device_id={"blk": (q + dq) % n}, device_id_type=MESH)
                copy.start()
                sends.append(copy)
    for copy in code_copies:
        copy.wait()
    table = all_ref[:, 0, :]
    ours = jnp.logical_and(table >= team * cube, table < (team + 1) * cube).astype(jnp.int32)
    inner = table - team * cube
    group_ids = lax.broadcasted_iota(jnp.int32, (groups, 1), 0)
    totals = jnp.sum(ours, axis=1, keepdims=True)
    before = jnp.zeros((groups, 1), jnp.int32)
    for other in range(groups):
        before += jnp.where(group_ids > other, totals[other:other + 1], 0)
    size = groups // teams // 2
    member = g // 2 % size
    places = lax.broadcasted_iota(jnp.int32, (groups, list_ref.shape[1]), 1) * size + member
    listed = jnp.zeros(places.shape, jnp.int32)
    for slot in range(slots):
        column = ours[:, slot:slot + 1]
        value = (group_ids * slots + slot) * cube + inner[:, slot:slot + 1]
        rank = jnp.where(column > 0, before, -1)
        listed += jnp.where(places == rank, value, 0)
        before += column
    list_ref[...] = jnp.sum(listed, axis=0, keepdims=True)
    whole = jnp.sum(totals, axis=0, keepdims=True)
    count_ref[...] = jnp.broadcast_to((whole - member + size - 1) // size, count_ref.shape)

    forwards = []
    at = 0
    for m in range(runs):
        for x, (src, dst) in enumerate(arrays):
            for dq in range(1, n):
                sends[at].wait_recv()
                at += 1
                piece = dst.at[((q + n - dq) % n) * runs + m, mine]
                copy = pltpu.make_async_remote_copy(
                    src_ref=piece, dst_ref=piece,
                    send_sem=fsend_sem.at[m, x, dq - 1], recv_sem=frecv_sem.at[m, x, dq - 1],
                    device_id={"grp": partner}, device_id_type=MESH)
                copy.start()
                forwards.append(copy)
    held.wait()
    for copy in sends:
        copy.wait_send()
    for copy in forwards:
        copy.wait()


def compute_kernel(groups, slots, teams, occupied, listed, counts, singles, occ, vir, integrals_ref, dp_ref, cp_ref,
                   row_ref, out_ref, vbc_ref, cf_ref):
    q = lax.axis_index("blk")
    core = lax.axis_index("grp") % 2
    blocks, width = integrals_ref.shape[1], integrals_ref.shape[2]
    count = counts[0, 0]
    last = listed.shape[1] - 1
    quads = blocks // 4
    per = max(1, 8 // quads)
    total_steps = per * quads
    lag, ranges = 2, 4

    across = jnp.broadcast_to(row_ref[...], (width, width))
    vbc_ref[...] = across + across.T
    cf_ref[...] = cp_ref[...].astype(jnp.float32)
    out_ref[...] = jnp.zeros_like(out_ref)
    rows = lax.broadcasted_iota(jnp.int32, out_ref.shape, 0)
    lanes = lax.broadcasted_iota(jnp.int32, out_ref.shape, 1)

    def decode(at):
        code = listed[0, jnp.minimum(at, last)]
        k = lax.rem(code, occupied)
        j = lax.rem(lax.div(code, occupied), occupied)
        i = lax.rem(lax.div(code, occupied * occupied), occupied)
        return i, j, k, lax.div(j * occupied + k, teams), lax.div(k * occupied + j, teams)

    def run(*accs):
        acc = [[accs[(x * ranges + r) * 2:(x * ranges + r) * 2 + 2] for r in range(ranges)] for x in range(2)]

        def push(at, quad, reg):
            i, _, _, _, kj = decode(at)
            for x in range(2):
                a = 4 * quad + 2 * x
                top = jnp.concatenate([dp_ref[kj], integrals_ref[i, a]], axis=1)
                low = jnp.concatenate([dp_ref[kj], integrals_ref[i, a + 1]], axis=1)
                pltpu.matmul_push_rhs(jnp.concatenate([top, low], axis=0), staging_register=reg, mxu_index=x, transpose=True)

        def multiply(at, quad, reg, r):
            i, _, _, jk, _ = decode(at)
            for h in range(2):
                for x in range(2):
                    left = jnp.concatenate([integrals_ref[i, 4 * quad + 2 * x + h], dp_ref[jk]], axis=1)
                    pltpu.matmul_acc_lhs(acc[x][r][h], left, load_staged_rhs=reg if h == 0 else None)

        def gather_up(at, quad, r, total):
            i, j, k, jk, _ = decode(at)
            occ_sum = occ[i] + occ[j] + occ[k]
            if quad == 0:
                total = jnp.zeros((8, width), jnp.float32)
            for h in range(2):
                for x in range(2):
                    a = core * blocks + 4 * quad + 2 * x + h
                    connected = pltpu.matmul_pop(acc[x][r][h])[:, h * width:(h + 1) * width]
                    full = connected + singles[i, a] * cf_ref[jk]
                    denominator = (occ_sum - vir[q * 2 * blocks + a]) - vbc_ref[...]
                    value = full * full / denominator
                    total = total + jnp.sum(value.reshape(width // 8, 8, width), axis=0)
            return total

        def settle(at, total):
            place = lax.div(listed[0, jnp.clip(at, 0, last)], occupied * occupied * occupied)
            real = jnp.logical_and(at >= 0, at < count)
            other, slot = jnp.where(real, lax.div(place, slots), -1), lax.rem(place, slots)
            here = jnp.logical_and(rows == other, lanes == slot)
            out_ref[...] += jnp.where(here, jnp.sum(total), 0.0)

        def finish(trip, step, total):
            at, quad = trip * per + step // quads, step % quads
            total = gather_up(jnp.maximum(at, 0), quad, step % ranges, total)
            if quad == quads - 1:
                settle(at, total)
            return total

        for side in acc:
            for pair in side:
                for one in pair:
                    pltpu.matmul_pop(one)
        push(0, 0, 0)

        def trip(b, total):
            for step in range(total_steps):
                multiply(b * per + step // quads, step % quads, step % 2, step % ranges)
                push(b * per + (step + 1) // quads, (step + 1) % quads, (step + 1) % 2)
                if step < lag:
                    total = finish(b - 1, total_steps + step - lag, total)
                else:
                    total = finish(b, step - lag, total)
            return total

        trips = lax.div(count + per - 1, per)
        total = lax.fori_loop(0, trips, trip, jnp.zeros((8, width), jnp.float32))
        for step in range(total_steps - lag, total_steps):
            total = finish(trips - 1, step, total)
        for x in range(2):
            pltpu.matmul_acc_lhs(acc[x][0][0], jnp.zeros((width, 2 * width), jnp.bfloat16), load_staged_rhs=0)
            pltpu.matmul_pop(acc[x][0][0])

    pl.run_scoped(run, *[pltpu.ACC(x)((width, 2 * width), jnp.float32) for x in range(2) for _ in range(2 * ranges)])


def reduce_kernel(n, groups, slots, part_ref, trip_ref, mean_ref, blk_buf, grp_buf, send_sem, recv_sem, gsend_sem, grecv_sem,
                  stage_ref):
    g = lax.axis_index("grp")
    q = lax.axis_index("blk")
    barrier = pltpu.get_barrier_semaphore()
    for dg in range(1, groups):
        pl.semaphore_signal(barrier, inc=1, device_id={"grp": (g + dg) % groups}, device_id_type=MESH)
    for dq in range(1, n):
        pl.semaphore_signal(barrier, inc=1, device_id={"blk": (q + dq) % n}, device_id_type=MESH)
    pl.semaphore_wait(barrier, groups - 1 + n - 1)
    copies = []
    for dq in range(1, n):
        copy = pltpu.make_async_remote_copy(
            src_ref=part_ref, dst_ref=blk_buf.at[q], send_sem=send_sem.at[dq - 1], recv_sem=recv_sem.at[dq - 1],
            device_id={"blk": (q + dq) % n}, device_id_type=MESH)
        copy.start()
        copies.append(copy)
    blk_buf[q] = part_ref[...]
    for copy in copies:
        copy.wait()
    stage = jnp.sum(blk_buf[...], axis=0)
    stage_ref[...] = stage
    grp_buf[g] = stage
    copies = []
    for dg in range(1, groups):
        copy = pltpu.make_async_remote_copy(
            src_ref=stage_ref, dst_ref=grp_buf.at[g], send_sem=gsend_sem.at[dg - 1], recv_sem=grecv_sem.at[dg - 1],
            device_id={"grp": (g + dg) % groups}, device_id_type=MESH)
        copy.start()
        copies.append(copy)
    for copy in copies:
        copy.wait()
    table = jnp.sum(grp_buf[...], axis=0)
    rows = lax.broadcasted_iota(jnp.int32, table.shape, 0)
    trip_ref[...] = jnp.sum(jnp.where(rows == g, table, 0.0), axis=0, keepdims=True)
    mean_ref[...] = jnp.sum(table, keepdims=True) / (groups * slots)


def body(n, groups, integrals, doubles, coulomb, singles, occ_energy, vir_energy, triplets, tile_count):
    occupied, _, width, _ = integrals.shape
    rows = doubles.shape[0]
    slots = triplets.shape[1]
    teams = team_count(occupied, rows, groups)
    runs = rows // teams
    pairs = n * runs
    f32, i32 = jnp.float32, jnp.int32
    vmem = pl.BlockSpec(memory_space=pltpu.VMEM)
    smem = pl.BlockSpec(memory_space=pltpu.SMEM)
    hbm = pl.BlockSpec(memory_space=pltpu.HBM)
    dma = pltpu.SemaphoreType.DMA

    row_bytes = pairs * width * width * doubles.dtype.itemsize
    spare = 1 << 20
    blocks = integrals.shape[1] // 2
    half = jax.ShapeDtypeStruct((occupied, blocks, width, width), integrals.dtype)
    keep = half.size * half.dtype.itemsize + 4 * row_bytes + 2 * spare
    lanes = -(-slots // 128) * 128
    length = -(-groups * slots // 128) * 128

    packed = jax.ShapeDtypeStruct((pairs, width, width), doubles.dtype)
    dp, cp, held, listed, counts = pl.pallas_call(
        functools.partial(gather_kernel, n, groups, teams, occupied, slots),
        out_shape=(packed, packed, half, jax.ShapeDtypeStruct((1, length), i32), jax.ShapeDtypeStruct((1, 128), i32)),
        in_specs=[hbm, hbm, hbm, hbm, smem],
        out_specs=(vmem, vmem, vmem, vmem, vmem),
        scratch_shapes=[
            pltpu.VMEM((groups, 1, lanes), i32), pltpu.VMEM((3, 1, slots), i32), dma, dma, dma((runs, 2)), dma((runs, 2, n - 1)), dma((runs, 2, n - 1)), dma((runs, 2, n - 1)), dma((runs, 2, n - 1)),
            dma((groups - 1,)), dma((groups - 1,)),
        ],
        compiler_params=pltpu.CompilerParams(collective_id=0, has_side_effects=True, vmem_limit_bytes=keep),
        name="gather",
    )(*(pltpu.with_memory_space_constraint(x, pltpu.HBM)
        for x in (doubles, coulomb, integrals, jnp.transpose(triplets, (2, 0, 1)))), tile_count)

    part = pl.pallas_call(
        functools.partial(compute_kernel, groups, slots, teams, occupied),
        out_shape=jax.ShapeDtypeStruct((groups, slots), f32),
        in_specs=[smem, smem, smem, smem, smem, vmem, vmem, vmem, vmem],
        out_specs=vmem,
        scratch_shapes=[pltpu.VMEM((width, width), f32), pltpu.VMEM((pairs, width, width), f32)],
        compiler_params=pltpu.CompilerParams(vmem_limit_bytes=keep),
        name="energy",
    )(listed, counts, singles, occ_energy, vir_energy, held, dp, cp, vir_energy.reshape(1, width))

    trip, mean = pl.pallas_call(
        functools.partial(reduce_kernel, n, groups, slots),
        out_shape=(jax.ShapeDtypeStruct((1, slots), f32), jax.ShapeDtypeStruct((1, 1), f32)),
        in_specs=[vmem],
        out_specs=(vmem, vmem),
        scratch_shapes=[
            pltpu.VMEM((n, groups, slots), f32), pltpu.VMEM((groups, groups, slots), f32),
            dma((n - 1,)), dma((n - 1,)), dma((groups - 1,)), dma((groups - 1,)), pltpu.VMEM((groups, slots), f32),
        ],
        compiler_params=pltpu.CompilerParams(collective_id=1, has_side_effects=True, vmem_limit_bytes=4 * spare),
        name="join",
    )(part)
    return trip, mean.reshape(())


def solution(mesh):
    in_specs = (
        P(None, "blk", None, None),
        P("blk", None, None),
        P("blk", None, None),
        P(None, "blk"),
        P(),
        P(),
        P("grp", None, None),
        P("grp"),
    )
    out_specs = (P("grp", None), P())
    step = functools.partial(body, mesh.shape["blk"], mesh.shape["grp"])
    return jax.shard_map(step, mesh=mesh, in_specs=in_specs, out_specs=out_specs, check_vma=False)
```

profile of v0, /device:TPU:0, one launch (start us, length us, event | category | flops | bytes accessed | tf_op | source)
XLA Modules:
  0.0 37.7 jit_solution(4673162797080506958)
XLA Ops:
  0.6 0.0 copy-start.1
  0.6 0.0 copy-start.2
  0.7 0.0 copy-start
  1.3 16.0 %gather.1 = (bf16[16,128,128]{2,1,0:T(8,128)(2,1)S(1)}, bf16[16,128,128]{2,1,0:T(8,128)(2,1)S(1)}, bf16[8,16,128,128]{3,2,1,0:T(8,128)(2,1)S(1)}, s32[1,128]{1,0:T(1,128)S(1)}, s32[1,128]{1,0:T(1,128)S(1)}) custom-call(bf16[16,128,128]{2,1,0:T(8,128)(2,1)} %doubles_ref.1, bf16[16,128,128]{2,1,0:T(8,128)(2,1)} %coulomb_ref.1, ...), custom_call_target="tpu_custom_call" | custom-call | tf_op jit(solution)/shard_map/gather/pallas_call | solution.py:287
  17.3 0.0 copy-done.1
  17.3 0.0 copy-done.2
  17.3 0.0 copy-done
  17.3 9.4 %energy.1.part_ref = f32[8,16]{1,0:T(8,128)S(1)} custom-call(s32[1,128]{1,0:T(1,128)S(1)} %get-tuple-element.9.listed, s32[1,128]{1,0:T(1,128)S(1)} %get-tuple-element.10.counts, f32[8,32]{1,0:T(8,128)S(1)} %copy-done, f32[8]{0:T(128)S(1)} %copy-done.2, f32[128]{0:T(128)S(1)} %copy-done.1, bf16[8,16,128,128]{3,2,1,0:T(8,128)(2,1)S(1)} %get-tuple-element.11.integrals_ref, ...), custom_call_target="tpu_custom_call" | custom-call | tf_op jit(solution)/shard_map/energy/pallas_call | solution.py:301
  26.8 8.7 %join.1 = (f32[1,16]{1,0:T(1,128)S(1)}, f32[1,1]{1,0:T(1,128)}) custom-call(f32[8,16]{1,0:T(8,128)S(1)} %energy.1.part_ref), custom_call_target="tpu_custom_call" | custom-call | tf_op jit(solution)/shard_map/join/pallas_call | solution.py:311
  35.5 0.5 %copy.13 = f32[1,16]{1,0:T(1,128)} copy(f32[1,16]{1,0:T(1,128)S(1)} %get-tuple-element.18) | data formatting | bytes 128
Async XLA Ops:
  0.6 16.7 %copy-start.1 = (f32[128]{0:T(128)S(1)}, f32[128]{0:T(128)}, u32[]{:S(2)}) copy-start(f32[128]{0:T(128)} %vir.1) | copy-start | bytes 1540
  0.6 16.7 %copy-start.2 = (f32[8]{0:T(128)S(1)}, f32[8]{0:T(128)}, u32[]{:S(2)}) copy-start(f32[8]{0:T(128)} %occ.1) | copy-start | bytes 100
  0.7 16.7 %copy-start = (f32[8,32]{1,0:T(8,128)S(1)}, f32[8,32]{1,0:T(8,128)}, u32[]{:S(2)}) copy-start(f32[8,32]{1,0:T(8,128)} %singles.1) | copy-start | bytes 3076
where the time goes:
time: 37.4 us; the launch traced here: 37.7 us
  Pallas kernels  34.1 us (91%)
  between operations  3.12 us (8%)
  local copies, waits for them, and re-layouts  0.53 us (1%)
    pallas_call x1, Pallas kernels, body(): pl.pallas_call(functools.partial(gather_kernel, n, groups, teams, occupie...  16 us
    pallas_call x1, Pallas kernels, body(): pl.pallas_call(functools.partial(compute_kernel, groups, slots, teams, oc...  9.42 us
    pallas_call x1, Pallas kernels, body(): pl.pallas_call(functools.partial(reduce_kernel, n, groups, slots), out_sh...  8.69 us

commit v1 on v0

--- a/solution.py
+++ b/solution.py
@@ -124,12 +124,12 @@
         copy.wait()
 
 
-def compute_kernel(groups, slots, teams, occupied, listed, counts, singles, occ, vir, integrals_ref, dp_ref, cp_ref,
+def compute_kernel(groups, slots, teams, occupied, fixed, listed, counts, singles, occ, vir, integrals_ref, dp_ref, cp_ref,
                    row_ref, out_ref, vbc_ref, cf_ref):
     q = lax.axis_index("blk")
     core = lax.axis_index("grp") % 2
     blocks, width = integrals_ref.shape[1], integrals_ref.shape[2]
-    count = counts[0, 0]
+    count = jnp.maximum(counts[0, 0] - fixed, 0)
     last = listed.shape[1] - 1
     quads = blocks // 4
     per = max(1, 8 // quads)
@@ -144,7 +144,7 @@
     lanes = lax.broadcasted_iota(jnp.int32, out_ref.shape, 1)
 
     def decode(at):
-        code = listed[0, jnp.minimum(at, last)]
+        code = listed[0, jnp.minimum(at + fixed, last)]
         k = lax.rem(code, occupied)
         j = lax.rem(lax.div(code, occupied), occupied)
         i = lax.rem(lax.div(code, occupied * occupied), occupied)
@@ -184,7 +184,7 @@
             return total
 
         def settle(at, total):
-            place = lax.div(listed[0, jnp.clip(at, 0, last)], occupied * occupied * occupied)
+            place = lax.div(listed[0, jnp.clip(at + fixed, 0, last)], occupied * occupied * occupied)
             real = jnp.logical_and(at >= 0, at < count)
             other, slot = jnp.where(real, lax.div(place, slots), -1), lax.rem(place, slots)
             here = jnp.logical_and(rows == other, lanes == slot)
@@ -224,8 +224,8 @@
     pl.run_scoped(run, *[pltpu.ACC(x)((width, 2 * width), jnp.float32) for x in range(2) for _ in range(2 * ranges)])
 
 
-def reduce_kernel(n, groups, slots, part_ref, trip_ref, mean_ref, blk_buf, grp_buf, send_sem, recv_sem, gsend_sem, grecv_sem,
-                  stage_ref):
+def reduce_kernel(n, groups, slots, teams, occupied, fixed, batch, listed, counts, singles, occ, vir, integrals_ref, dp_ref, cp_ref, row_ref,
+                  part_ref, trip_ref, mean_ref, blk_buf, grp_buf, send_sem, recv_sem, gsend_sem, grecv_sem, stage_ref, own_ref, vbc_ref):
     g = lax.axis_index("grp")
     q = lax.axis_index("blk")
     barrier = pltpu.get_barrier_semaphore()
@@ -233,15 +233,51 @@
         pl.semaphore_signal(barrier, inc=1, device_id={"grp": (g + dg) % groups}, device_id_type=MESH)
     for dq in range(1, n):
         pl.semaphore_signal(barrier, inc=1, device_id={"blk": (q + dq) % n}, device_id_type=MESH)
+
+    blocks, width = integrals_ref.shape[1], integrals_ref.shape[2]
+    first = (g % 2) * blocks
+    across = jnp.broadcast_to(row_ref[...], (width, width))
+    vbc_ref[...] = across + across.T
+    count = counts[0, 0]
+    spots = lax.broadcasted_iota(jnp.int32, part_ref.shape, 0) * slots + lax.broadcasted_iota(jnp.int32, part_ref.shape, 1)
+    contract = (((1,), (1,)), ((), ()))
+
+    def step(b, table):
+        for u in range(batch):
+            at = b * batch + u
+            code = listed[0, at]
+            k = lax.rem(code, occupied)
+            j = lax.rem(lax.div(code, occupied), occupied)
+            i = lax.rem(lax.div(code, occupied * occupied), occupied)
+            place = lax.div(code, occupied * occupied * occupied)
+            jk = lax.div(j * occupied + k, teams)
+            kj = lax.div(k * occupied + j, teams)
+            occ_sum = occ[i] + occ[j] + occ[k]
+            d_jk, d_kj = dp_ref[jk], dp_ref[kj]
+            total = jnp.zeros((8, width), jnp.float32)
+            for a in range(blocks):
+                block = integrals_ref[i, a]
+                left = jnp.concatenate([block, d_jk], axis=1)
+                right = jnp.concatenate([d_kj, block], axis=1)
+                connected = lax.dot_general(left, right, contract, preferred_element_type=jnp.float32)
+                full = connected + singles[i, first + a] * cp_ref[jk].astype(jnp.float32)
+                denominator = (occ_sum - vir[q * 2 * blocks + first + a]) - vbc_ref[...]
+                value = full * full / denominator
+                total = total + jnp.sum(value.reshape(width // 8, 8, width), axis=0)
+            here = jnp.logical_and(spots == place, at < count)
+            table = table + jnp.where(here, jnp.sum(total), 0.0)
+        return table
+
+    own_ref[...] = lax.fori_loop(0, fixed // batch, step, part_ref[...])
     pl.semaphore_wait(barrier, groups - 1 + n - 1)
     copies = []
     for dq in range(1, n):
         copy = pltpu.make_async_remote_copy(
-            src_ref=part_ref, dst_ref=blk_buf.at[q], send_sem=send_sem.at[dq - 1], recv_sem=recv_sem.at[dq - 1],
+            src_ref=own_ref, dst_ref=blk_buf.at[q], send_sem=send_sem.at[dq - 1], recv_sem=recv_sem.at[dq - 1],
             device_id={"blk": (q + dq) % n}, device_id_type=MESH)
         copy.start()
         copies.append(copy)
-    blk_buf[q] = part_ref[...]
+    blk_buf[q] = own_ref[...]
     for copy in copies:
         copy.wait()
     stage = jnp.sum(blk_buf[...], axis=0)
@@ -282,6 +318,7 @@
     keep = half.size * half.dtype.itemsize + 4 * row_bytes + 2 * spare
     lanes = -(-slots // 128) * 128
     length = -(-groups * slots // 128) * 128
+    fixed, batch = 8, 4
 
     packed = jax.ShapeDtypeStruct((pairs, width, width), doubles.dtype)
     dp, cp, held, listed, counts = pl.pallas_call(
@@ -299,7 +336,7 @@
         for x in (doubles, coulomb, integrals, jnp.transpose(triplets, (2, 0, 1)))), tile_count)
 
     part = pl.pallas_call(
-        functools.partial(compute_kernel, groups, slots, teams, occupied),
+        functools.partial(compute_kernel, groups, slots, teams, occupied, fixed),
         out_shape=jax.ShapeDtypeStruct((groups, slots), f32),
         in_specs=[smem, smem, smem, smem, smem, vmem, vmem, vmem, vmem],
         out_specs=vmem,
@@ -309,17 +346,18 @@
     )(listed, counts, singles, occ_energy, vir_energy, held, dp, cp, vir_energy.reshape(1, width))
 
     trip, mean = pl.pallas_call(
-        functools.partial(reduce_kernel, n, groups, slots),
+        functools.partial(reduce_kernel, n, groups, slots, teams, occupied, fixed, batch),
         out_shape=(jax.ShapeDtypeStruct((1, slots), f32), jax.ShapeDtypeStruct((1, 1), f32)),
-        in_specs=[vmem],
+        in_specs=[smem, smem, smem, smem, smem, vmem, vmem, vmem, vmem, vmem],
         out_specs=(vmem, vmem),
         scratch_shapes=[
             pltpu.VMEM((n, groups, slots), f32), pltpu.VMEM((groups, groups, slots), f32),
             dma((n - 1,)), dma((n - 1,)), dma((groups - 1,)), dma((groups - 1,)), pltpu.VMEM((groups, slots), f32),
+            pltpu.VMEM((groups, slots), f32), pltpu.VMEM((width, width), f32),
         ],
-        compiler_params=pltpu.CompilerParams(collective_id=1, has_side_effects=True, vmem_limit_bytes=4 * spare),
+        compiler_params=pltpu.CompilerParams(collective_id=1, has_side_effects=True, vmem_limit_bytes=keep),
         name="join",
-    )(part)
+    )(listed, counts, singles, occ_energy, vir_energy, held, dp, cp, vir_energy.reshape(1, width), part)
     return trip, mean.reshape(())
 
 

time: 37.4 us -> 37.4 us (level)
    pallas_call x1, Pallas kernels: 9.42 us -> 6.86 us  [body(): pl.pallas_call(functools.partial(compute_kernel, groups, slots, teams, oc...]
    pallas_call x1, Pallas kernels: 8.69 us -> 10.9 us  [body(): pl.pallas_call(functools.partial(reduce_kernel, n, groups, slots, teams,...]
where the time goes in v1:
time: 37.4 us
  Pallas kernels  33.8 us (90%)
  between operations  3.12 us (8%)
  local copies, waits for them, and re-layouts  0.53 us (1%)
    pallas_call x1, Pallas kernels, body(): pl.pallas_call(functools.partial(gather_kernel, n, groups, teams, occupie...  16 us
    pallas_call x1, Pallas kernels, body(): pl.pallas_call(functools.partial(reduce_kernel, n, groups, slots, teams,...  10.9 us
    pallas_call x1, Pallas kernels, body(): pl.pallas_call(functools.partial(compute_kernel, groups, slots, teams, oc...  6.86 us

profile of v1, /device:TPU:0, one launch (start us, length us, event | category | flops | bytes accessed | tf_op | source)
XLA Modules:
  0.0 37.4 jit_solution(759488170076585248)
XLA Ops:
  0.6 0.0 copy-start.1
  0.6 0.0 copy-start.2
  0.7 0.0 copy-start
  1.3 16.0 %gather.1 = (bf16[16,128,128]{2,1,0:T(8,128)(2,1)S(1)}, bf16[16,128,128]{2,1,0:T(8,128)(2,1)S(1)}, bf16[8,16,128,128]{3,2,1,0:T(8,128)(2,1)S(1)}, s32[1,128]{1,0:T(1,128)S(1)}, s32[1,128]{1,0:T(1,128)S(1)}) custom-call(bf16[16,128,128]{2,1,0:T(8,128)(2,1)} %doubles_ref.1, bf16[16,128,128]{2,1,0:T(8,128)(2,1)} %coulomb_ref.1, ...), custom_call_target="tpu_custom_call" | custom-call | tf_op jit(solution)/shard_map/gather/pallas_call | solution.py:324
  17.3 0.0 copy-done.1
  17.3 0.0 copy-done.2
  17.3 0.0 copy-done
  17.3 6.9 %energy.1.part_ref = f32[8,16]{1,0:T(8,128)S(1)} custom-call(s32[1,128]{1,0:T(1,128)S(1)} %get-tuple-element.9.listed, s32[1,128]{1,0:T(1,128)S(1)} %get-tuple-element.10.counts, f32[8,32]{1,0:T(8,128)S(1)} %copy-done, f32[8]{0:T(128)S(1)} %copy-done.2, f32[128]{0:T(128)S(1)} %copy-done.1, bf16[8,16,128,128]{3,2,1,0:T(8,128)(2,1)S(1)} %get-tuple-element.11.integrals_ref, ...), custom_call_target="tpu_custom_call" | custom-call | tf_op jit(solution)/shard_map/energy/pallas_call | solution.py:338
  24.2 10.9 %join.1 = (f32[1,16]{1,0:T(1,128)S(1)}, f32[1,1]{1,0:T(1,128)}) custom-call(s32[1,128]{1,0:T(1,128)S(1)} %get-tuple-element.9.listed, s32[1,128]{1,0:T(1,128)S(1)} %get-tuple-element.10.counts, f32[8,32]{1,0:T(8,128)S(1)} %copy-done, f32[8]{0:T(128)S(1)} %copy-done.2, f32[128]{0:T(128)S(1)} %copy-done.1, ...), custom_call_target="tpu_custom_call" | custom-call | tf_op jit(solution)/shard_map/join/pallas_call | solution.py:348
  35.2 0.5 %copy.13 = f32[1,16]{1,0:T(1,128)} copy(f32[1,16]{1,0:T(1,128)S(1)} %get-tuple-element.18) | data formatting | bytes 128
Async XLA Ops:
  0.6 16.7 %copy-start.1 = (f32[128]{0:T(128)S(1)}, f32[128]{0:T(128)}, u32[]{:S(2)}) copy-start(f32[128]{0:T(128)} %vir.3) | copy-start | bytes 1540
  0.6 16.7 %copy-start.2 = (f32[8]{0:T(128)S(1)}, f32[8]{0:T(128)}, u32[]{:S(2)}) copy-start(f32[8]{0:T(128)} %occ.3) | copy-start | bytes 100
  0.7 16.7 %copy-start = (f32[8,32]{1,0:T(8,128)S(1)}, f32[8,32]{1,0:T(8,128)}, u32[]{:S(2)}) copy-start(f32[8,32]{1,0:T(8,128)} %singles.3) | copy-start | bytes 3076
